TPU v7x, 32 devices: a whole 2x2x4 slice. The times are simulated.
32 devices in a mesh: samp: 16 (over z, y, x), tile: 2 (over core).
Axes of the slice: x: 2, y: 2, z: 4, core: 2. Of those that a mesh axis runs over, the one named last changes fastest.
Arguments:
- traits: bfloat16 [16384, 1024], P('samp'), may hold values from -300 to 300
- covariates: bfloat16 [16384, 32], P('samp'), may hold values from -6 to 6
- genotypes: int32 [16384, 512], P('samp', 'tile'), may hold values from 0 to 2
- shuffles: int32 [6, 16384], P(None, 'samp'), may hold values from 0 to 16383, as said below
Outputs:
- observed: float32 [1024, 512], P('samp', 'tile')
- perm_max: float32 [6, 1024], P(None, 'samp')
Inputs may be any that keep to these rules, and one draw needn't show every extreme that they name: Row p of shuffles maps each aligned block of 1024 samples one to one onto the same block's samples.
All inputs are finite; a program needn't handle non-finite values.
Results may differ from a plain program's by a relative error of at most 0.0045.
Values sent between devices are 32-bit elements; how exact they have to be, the bound alone decides.
A program may use at most 64 MiB of HBM per device.

v0:
```python
import math

import jax
import jax.numpy as jnp
from jax import lax
from jax.sharding import PartitionSpec as P

C = 32


epsilon = 1e-05


def cholesky_solve(factor, rhs):
    first = lax.linalg.triangular_solve(factor, rhs, left_side=True, lower=True)
    return lax.linalg.triangular_solve(factor, first, left_side=True, lower=True, transpose_a=True)


def cross_local(left, right):
    return lax.dot_general(
        left, right, (((0,), (0,)), ((), ())), preferred_element_type=jnp.float32
    )


def shards(traits, covariates, genotypes, shuffles):
    groups = lax.axis_size("samp")
    own_index = lax.axis_index("samp")
    local_rows = traits.shape[0]
    samples = local_rows * groups
    share_rows = traits.shape[1] // groups
    ones = jnp.ones((local_rows, 1), jnp.bfloat16)
    design = jnp.concatenate([ones, covariates], axis=1)
    dosage = genotypes.astype(jnp.bfloat16)
    gram = cross_local(design, design)
    xty = cross_local(design, traits)
    xtg = cross_local(design, dosage)
    gram, xty, xtg = lax.psum((gram, xty, xtg), "samp")
    factor = jnp.linalg.cholesky(gram)
    coef_traits = cholesky_solve(factor, xty).astype(jnp.bfloat16)
    coef_geno = cholesky_solve(factor, xtg).astype(jnp.bfloat16)
    resid_traits = traits.astype(jnp.float32) - jnp.dot(
        design, coef_traits, preferred_element_type=jnp.float32
    )
    resid_geno = dosage.astype(jnp.float32) - jnp.dot(
        design, coef_geno, preferred_element_type=jnp.float32
    )
    sum_traits, sum_geno = lax.psum(
        (jnp.sum(resid_traits * resid_traits, axis=0), jnp.sum(resid_geno * resid_geno, axis=0)),
        "samp",
    )
    mean_traits = sum_traits / samples
    mean_geno = sum_geno / samples
    rt_rows = resid_traits.astype(jnp.bfloat16)
    rg_rows = resid_geno.astype(jnp.bfloat16)
    scale_traits = lax.rsqrt(mean_traits + epsilon)
    scale_geno = lax.rsqrt(mean_geno + epsilon)
    factor_z = math.sqrt(samples - C - 2) / samples
    own_scale = lax.dynamic_slice_in_dim(scale_traits, own_index * share_rows, share_rows, 0)

    def owned_scores(trait_rows):
        summed = lax.psum(cross_local(trait_rows, rg_rows), "samp")
        owned = lax.dynamic_slice_in_dim(summed, own_index * share_rows, share_rows, 0)
        return owned * own_scale[:, None] * scale_geno[None, :] * factor_z

    observed = owned_scores(rt_rows)
    peaks = []
    for perm_id in range(shuffles.shape[0]):
        local_order = shuffles[perm_id] - own_index * local_rows
        shuffled = jnp.take(rt_rows, local_order, axis=0)
        peak = jnp.max(jnp.abs(owned_scores(shuffled)), axis=1)
        peak = lax.pmax(peak, "tile")
        peaks.append(peak)
    perm_max = jnp.stack(peaks, axis=0)
    return (observed, perm_max)


def solution(mesh):
    placed = (P("samp", None), P("samp", None), P("samp", "tile"), P(None, "samp"))
    return jax.shard_map(
        shards,
        mesh=mesh,
        in_specs=placed,
        out_specs=(P("samp", "tile"), P(None, "samp")),
        check_vma=False,
    )
```

profile of v0, /device:TPU:0, one launch (start us, length us, event | category | flops | bytes accessed | tf_op | source)
XLA Modules:
  0.0 421.3 jit_solution(16171988681237372863)
XLA Ops:
  7.2 2.8 fusion.31
  10.5 0.2 fusion.25
  10.7 78.7 %all-reduce.2 = (f32[33,33]{0,1:T(8,128)S(1)}, f32[33,256]{1,0:T(8,128)S(1)}) all-reduce(f32[33,33]{0,1:T(8,128)S(1)} %fusion.33, f32[33,256]{1,0:T(8,128)S(1)} %fusion.25), channel_id=1, replica_groups=mesh['samp'=16,'tile'=2] {'samp'}, use_global_device_ids=true, to_apply=%region_0.0 | all-reduce | flops 9537 | bytes 76296 | tf_op jit(solution)/shard_map/psum | solution.py:37
  89.5 3.0 cholesky.16
  92.6 0.6 compare_reduce_fusion
  93.2 0.7 fusion.35
  93.9 2.5 custom-call.12
  96.4 0.2 fusion.37
  96.7 0.2 convolution_convert_fusion.1
  96.8 0.4 multiply_reduce_fusion.1
  97.3 26.2 %all-reduce.8.cloned.1.call-done = f32[33,1024]{1,0:T(8,128)} async-done(((f32[33,1024]{1,0:T(8,128)}), f32[33,1024]{1,0:T(8,128)}) %all-reduce.8.cloned.1.call-update) | async-done | bytes 135184 | tf_op jit(solution)/shard_map/psum | solution.py:37
  123.4 1.3 fusion.40
  124.7 0.3 convolution_convert_fusion
  125.0 2.4 multiply_reduce_fusion
  127.4 1.8 fusion.60
  129.2 5.4 %gather_fusion.5 = bf16[1024,1024]{1,0:T(8,128)(2,1)} fusion(bf16[1024,1024]{1,0:T(8,128)(2,1)S(1)} %get-tuple-element.27, s32[1024]{0:T(1024)S(1)} %fusion.48), kind=kCustom, calls=%fused_computation.5.clone | custom fusion | bytes 4198400 | tf_op jit(solution)/shard_map/jit(_take)/gather | solution.py:69
  134.6 5.4 %gather_fusion.4 = bf16[1024,1024]{1,0:T(8,128)(2,1)} fusion(bf16[1024,1024]{1,0:T(8,128)(2,1)S(1)} %get-tuple-element.27, s32[1024]{0:T(1024)S(1)} %fusion.47), kind=kCustom, calls=%fused_computation.4.clone | custom fusion | bytes 4198400 | tf_op jit(solution)/shard_map/jit(_take)/gather | solution.py:69
  139.9 5.4 %gather_fusion.3 = bf16[1024,1024]{1,0:T(8,128)(2,1)} fusion(bf16[1024,1024]{1,0:T(8,128)(2,1)S(1)} %get-tuple-element.27, s32[1024]{0:T(1024)S(1)} %fusion.46), kind=kCustom, calls=%fused_computation.3.clone | custom fusion | bytes 4198400 | tf_op jit(solution)/shard_map/jit(_take)/gather | solution.py:69
  145.3 5.4 %gather_fusion.2 = bf16[1024,1024]{1,0:T(8,128)(2,1)} fusion(bf16[1024,1024]{1,0:T(8,128)(2,1)S(1)} %get-tuple-element.27, s32[1024]{0:T(1024)S(1)} %fusion.45), kind=kCustom, calls=%fused_computation.2.clone | custom fusion | bytes 4198400 | tf_op jit(solution)/shard_map/jit(_take)/gather | solution.py:69
  150.7 5.4 %gather_fusion.1 = bf16[1024,1024]{1,0:T(8,128)(2,1)} fusion(bf16[1024,1024]{1,0:T(8,128)(2,1)S(1)} %get-tuple-element.27, s32[1024]{0:T(1024)S(1)} %fusion.44), kind=kCustom, calls=%fused_computation.1.clone | custom fusion | bytes 4198400 | tf_op jit(solution)/shard_map/jit(_take)/gather | solution.py:69
  156.1 5.4 %gather_fusion = bf16[1024,1024]{1,0:T(8,128)(2,1)} fusion(bf16[1024,1024]{1,0:T(8,128)(2,1)S(1)} %get-tuple-element.27, s32[1024]{0:T(1024)S(1)} %fusion.43), kind=kCustom, calls=%fused_computation.clone | custom fusion | bytes 4198400 | tf_op jit(solution)/shard_map/jit(_take)/gather | solution.py:69
  161.4 3.7 fusion.1
  165.1 2.1 fusion.3
  167.2 2.0 fusion.5
  169.2 2.0 fusion.7
  171.2 2.0 fusion.9
  173.1 2.0 fusion.11
  175.2 43.9 %all-reduce.1 = (f32[256]{0:T(256)S(1)}, f32[1024]{0:T(1024)S(1)}) all-reduce(f32[256]{0:T(256)S(1)} %get-tuple-element.28, f32[1024]{0:T(1024)S(1)} %get-tuple-element.26), channel_id=1, replica_groups=mesh['samp'=16,'tile'=2] {'samp'}, use_global_device_ids=true, to_apply=%region_9.10 | all-reduce | flops 1280 | bytes 10240 | tf_op jit(solution)/shard_map/psum | solution.py:47
  219.2 190.2 %all-reduce.10.cloned.1.call-done = (f32[1024,256]{1,0:T(8,128)}, f32[1024,256]{1,0:T(8,128)}, f32[1024,256]{1,0:T(8,128)}, f32[1024,256]{1,0:T(8,128)}, f32[102...) async-done(((f32[1024,256]{1,0:T(8,128)}, f32[1024,256]{1,0:T(8,128)}, f32[1024,256]{1,0:T(8,128)}, f32[1024,256]{1,0:T(8,128)}, f32[1024,256]{1,0:T(8,128)}, ...) | async-done | bytes 7340048 | tf_op jit(solution)/shard_map/psum | solution.py:61
  409.4 1.9 abs_reduce_fusion
  411.3 2.5 all-reduce.4
  413.8 0.6 stack.27
  (40 shorter events, 0.6 us)
Async XLA Ops:
  7.2 3.0 copy-start.6
  7.2 3.2 copy-start.7
  7.2 3.3 copy-start
  7.2 116.2 %all-reduce.8.cloned.1.call-start = ((), (), s32[]{:S(2)}) async-start(), calls=%async_computation | async-start | bytes 327680 | tf_op jit(solution)/shard_map/psum | solution.py:37
  10.1 399.3 %all-reduce.10.cloned.1.call-start = ((), (), s32[]{:S(2)}) async-start(), calls=%async_computation.1 | async-start | bytes 14680064 | tf_op jit(solution)/shard_map/psum | solution.py:61
  161.4 3.7 copy-start.5
  165.1 2.1 copy-start.4
  167.2 2.0 copy-start.3
  169.2 2.0 copy-start.2
  171.2 2.0 copy-start.1
Sparse Core Ops, SparseCore 0:
  13.3 110.0 all-reduce.7
  175.3 234.0 all-reduce.9
where the time goes:
time: 422 us; the launch traced here: 421 us
  waiting for transfers between devices  216 us (51%)
  blocking collectives  125 us (30%)
  local copies, waits for them, and re-layouts  33 us (8%)
  matrix products  23.5 us (6%)
  between operations  14.3 us (3%)
  other arithmetic  8.93 us (2%)
    psum x1, waiting for transfers between devices, owned_scores(): summed = lax.psum(cross_local(trait_rows, rg_rows), 'samp')  190 us
    psum x1, blocking collectives, shards(): gram, xty, xtg = lax.psum((gram, xty, xtg), 'samp')  78.7 us
    psum x1, blocking collectives, shards(): lax.psum((jnp.sum(resid_traits * resid_traits, axis=0), jnp.sum(resid_gen...  43.9 us
    gather x6, local copies, waits for them, and re-layouts, shards(): shuffled = jnp.take(rt_rows, local_order, axis=0)  32.2 us
    psum x1, waiting for transfers between devices, shards(): gram, xty, xtg = lax.psum((gram, xty, xtg), 'samp')  26.2 us
    dot_general x10, matrix products, cross_local(): lax.dot_general(left, right, (((0,), (0,)), ((), ())), preferred_element_...  18.7 us
  transfers between devices with their start and end apart: 2, of which 2 were waited for; matrix products, arithmetic and copies ran while one was open for 2% of the time, Pallas kernels for 0%

commit v1 on v0

v1 whole, which is shorter than its diff:
```python
import functools
import math

import jax
import jax.numpy as jnp
from jax import lax
from jax.experimental import pallas as pl
from jax.experimental.pallas import tpu as pltpu
from jax.sharding import PartitionSpec as P

MESH = pl.DeviceIdType.MESH
LANES = 128
F32, BF16 = jnp.float32, jnp.bfloat16
epsilon = 1e-05

ORDERS = ((2, 1, 0), (1, 2, 0))


def grid_of(groups):
    x = 4 if groups % 32 == 0 else 2
    y = 2
    return (groups // (x * y), y, x)


def enter(me, groups):
    barrier = pltpu.get_barrier_semaphore()
    for d in range(1, groups):
        pl.semaphore_signal(
            barrier, inc=1, device_id={"samp": lax.rem(me + d, groups)}, device_id_type=MESH
        )
    return barrier


def gram_kernel(
    groups, dt_ref, d_ref, t_ref, g_ref, out_ref, parts, landed, mine, full, send, recv, send2, recv2
):
    me = lax.axis_index("samp")
    rows = dt_ref.shape[0]
    barrier = enter(me, groups)
    quota = parts.shape[0] // groups
    tile = 0

    def put(block):
        nonlocal tile
        for c in range(block.shape[1] // LANES):
            for r in range(rows // 8):
                parts[tile] = block[8 * r : 8 * r + 8, LANES * c : LANES * c + LANES]
                tile += 1

    dt = dt_ref[...]
    put(jnp.dot(dt, t_ref[...], preferred_element_type=F32))
    put(jnp.dot(dt, g_ref[...].astype(F32).astype(BF16), preferred_element_type=F32))
    put(jnp.dot(dt, d_ref[...], preferred_element_type=F32))
    used = tile
    for i in range(used, parts.shape[0]):
        parts[i] = jnp.zeros((8, LANES), F32)
    pl.semaphore_wait(barrier, groups - 1)
    copies = []
    for d in range(1, groups):
        peer = lax.rem(me + d, groups)
        copy = pltpu.make_async_remote_copy(
            src_ref=parts.at[pl.ds(peer * quota, quota)],
            dst_ref=landed.at[d - 1],
            send_sem=send.at[d - 1],
            recv_sem=recv.at[d - 1],
            device_id={"samp": peer},
            device_id_type=MESH,
        )
        copy.start()
        copies.append(copy)
    total = parts[pl.ds(me * quota, quota)]
    for d in range(1, groups):
        copies[d - 1].wait_recv()
        total = total + landed[d - 1]
    mine[...] = total
    full[pl.ds(me * quota, quota)] = total
    for d in range(1, groups):
        peer = lax.rem(me + d, groups)
        copy = pltpu.make_async_remote_copy(
            src_ref=mine,
            dst_ref=full.at[pl.ds(me * quota, quota)],
            send_sem=send2.at[d - 1],
            recv_sem=recv2.at[d - 1],
            device_id={"samp": peer},
            device_id_type=MESH,
        )
        copy.start()
        copies.append(copy)
    for d in range(1, groups):
        copies[groups - 2 + d].wait_recv()
    for i in range(used):
        c, r = divmod(i, rows // 8)
        out_ref[8 * r : 8 * r + 8, LANES * c : LANES * c + LANES] = full[i]
    for copy in copies:
        copy.wait_send()


def cross_products(design_t, design, traits, genotypes, groups):
    rows = design_t.shape[0]
    width = traits.shape[1] + genotypes.shape[1] + design.shape[1]
    tiles = rows // 8 * (width // LANES)
    quota = -(-tiles // groups)
    vmem = pl.BlockSpec(memory_space=pltpu.VMEM)
    sems = pltpu.SemaphoreType.DMA((groups - 1,))
    return pl.pallas_call(
        functools.partial(gram_kernel, groups),
        out_shape=jax.ShapeDtypeStruct((rows, width), F32),
        in_specs=[vmem] * 4,
        out_specs=vmem,
        scratch_shapes=[
            pltpu.VMEM((quota * groups, 8, LANES), F32),
            pltpu.VMEM((groups - 1, quota, 8, LANES), F32),
            pltpu.VMEM((quota, 8, LANES), F32),
            pltpu.VMEM((quota * groups, 8, LANES), F32),
            sems,
            sems,
            sems,
            sems,
        ],
        compiler_params=pltpu.CompilerParams(collective_id=0, has_side_effects=True),
        name="gram",
    )(design_t, design, traits, genotypes)


def scan_kernel(
    dims, samples, d_ref, t_ref, g_ref, ct_ref, cg_ref, order_ref, score_ref, peak_ref, square_ref,
    rt, rg, moved, prod, squares, sq_send, sq_recv, send, recv, *bufs
):
    groups = dims[0] * dims[1] * dims[2]
    me = lax.axis_index("samp")
    here = (me // (dims[1] * dims[2]), lax.rem(me // dims[2], dims[1]), lax.rem(me, dims[2]))
    turns, n_parts = prod.shape[0], prod.shape[1]
    share, width = prod.shape[5], prod.shape[6]
    local, traits = t_ref.shape
    barrier = enter(me, groups)

    step = min(256, local)
    sq_t = jnp.zeros((1, traits), F32)
    sq_g = jnp.zeros((1, width), F32)
    for i in range(local // step):
        at = slice(i * step, (i + 1) * step)
        d = d_ref[at, :]
        resid = t_ref[at, :].astype(F32) - jnp.dot(d, ct_ref[...], preferred_element_type=F32)
        sq_t = sq_t + jnp.sum(resid * resid, axis=0, keepdims=True)
        rt[:, at] = resid.astype(BF16).T
        dose = g_ref[at, :].astype(F32)
        resid = dose - jnp.dot(d, cg_ref[...], preferred_element_type=F32)
        sq_g = sq_g + jnp.sum(resid * resid, axis=0, keepdims=True)
        rg[at, :] = resid.astype(BF16)
    squares[0] = jnp.zeros(squares.shape[1:], F32)
    n_t = traits // LANES
    for c in range(n_t):
        squares[0, c : c + 1, :] = sq_t[:, c * LANES : (c + 1) * LANES]
    for c in range(width // LANES):
        squares[0, n_t + c : n_t + c + 1, :] = sq_g[:, c * LANES : (c + 1) * LANES]
    pl.semaphore_wait(barrier, groups - 1)

    def square_copy(d):
        return pltpu.make_async_remote_copy(
            src_ref=squares.at[0],
            dst_ref=squares.at[d],
            send_sem=sq_send.at[d - 1],
            recv_sem=sq_recv.at[d - 1],
            device_id={"samp": lax.rem(me + d, groups)},
            device_id_type=MESH,
        )

    def spot(axis, d):
        j = lax.rem(here[axis] + d, dims[axis])
        at = list(here)
        at[axis] = j
        return j, (at[0] * dims[1] + at[1]) * dims[2] + at[2]

    def pick(axis, order, stage, j):
        left = [a for a in (0, 1, 2) if a not in order[:stage]]
        return tuple(j if a == axis else slice(None) for a in left)

    def source(k, p, stage):
        if stage == 0:
            return prod.at[k, p]
        return bufs[5 * p + 2 * stage - 1].at[k]

    def copies(k, p, stage):
        order = ORDERS[p]
        axis = order[stage]
        first = sum(dims[a] - 1 for a in order[:stage])
        out = []
        for d in range(1, dims[axis]):
            j, peer = spot(axis, d)
            out.append(
                pltpu.make_async_remote_copy(
                    src_ref=source(k, p, stage).at[pick(axis, order, stage, j)],
                    dst_ref=bufs[5 * p + 2 * stage].at[k, d - 1],
                    send_sem=send.at[k, p, first + d - 1],
                    recv_sem=recv.at[k, p, first + d - 1],
                    device_id={"samp": peer},
                    device_id_type=MESH,
                )
            )
        return out

    def begin(k, stage):
        for p in range(n_parts):
            for copy in copies(k, p, stage):
                copy.start()

    def collect(k, stage):
        for p in range(n_parts):
            order = ORDERS[p]
            axis = order[stage]
            for copy in copies(k, p, stage):
                copy.wait_recv()
            total = source(k, p, stage)[pick(axis, order, stage, here[axis])]
            for d in range(1, dims[axis]):
                total = total + bufs[5 * p + 2 * stage][k, d - 1]
            if stage < 2:
                bufs[5 * p + 2 * stage + 1][k] = total
            else:
                score_ref[k, p * share : (p + 1) * share, :] = total

    def multiply(k):
        order = order_ref[pl.ds(k, 1), :]
        for i in range(local // step):
            row = lax.broadcasted_iota(jnp.int32, (step, local), 0) + i * step
            hot = jnp.where(row == order, 1.0, 0.0).astype(BF16)
            moved[i * step : (i + 1) * step, :] = jnp.dot(
                hot, rg[...], preferred_element_type=F32
            ).astype(BF16)
        depth = traits // dims[0]
        for z in range(dims[0]):
            block = jnp.dot(
                rt[z * depth : (z + 1) * depth, :], moved[...], preferred_element_type=F32
            ).reshape(dims[1], dims[2], n_parts, share, width)
            for p in range(n_parts):
                prod[k, p, z] = block[:, :, p]

    def turn(t, carry):
        @pl.when(t < turns)
        def _():
            multiply(t)
            begin(t, 0)

        @pl.when(t == 0)
        def _():
            for d in range(1, groups):
                square_copy(d).start()

        for stage in range(3):
            k = t - 1 - stage

            @pl.when(jnp.logical_and(k >= 0, k < turns))
            def _():
                collect(k, stage)
                if stage < 2:
                    begin(k, stage + 1)

        return carry

    lax.fori_loop(0, turns + 3, turn, 0)

    total = squares[0]
    for d in range(1, groups):
        square_copy(d).wait_recv()
        total = total + squares[d]
    square_ref[...] = total
    gain = lax.rsqrt(total / samples + epsilon)
    gain = jnp.concatenate([gain[n_t + c : n_t + c + 1, :] for c in range(width // LANES)], axis=1)
    for k in range(turns):
        scaled = score_ref[k] * gain
        score_ref[k] = scaled
        peak_ref[k] = jnp.broadcast_to(
            jnp.max(jnp.abs(scaled), axis=1, keepdims=True), peak_ref.shape[1:]
        )

    def finish(k, carry):
        for p in range(n_parts):
            for stage in range(3):
                for copy in copies(k, p, stage):
                    copy.wait_send()
        return carry

    lax.fori_loop(0, turns, finish, 0)
    for d in range(1, groups):
        square_copy(d).wait_send()


def scan(design, traits, genotypes, coef_t, coef_g, orders, groups):
    dims = grid_of(groups)
    turns = orders.shape[0]
    local, n_traits = traits.shape
    width = genotypes.shape[1]
    own = n_traits // groups
    n_parts = len(ORDERS)
    share = own // n_parts
    bufs = []
    for order in ORDERS:
        left = [0, 1, 2]
        for stage, axis in enumerate(order):
            left.remove(axis)
            rest = tuple(dims[a] for a in left) + (share, width)
            bufs.append(pltpu.VMEM((turns, dims[axis] - 1) + rest, F32))
            if stage < 2:
                bufs.append(pltpu.VMEM((turns,) + rest, F32))
    hops = sum(n - 1 for n in dims)
    rows = -(-(n_traits + width) // (8 * LANES)) * 8
    vmem = pl.BlockSpec(memory_space=pltpu.VMEM)
    sems = pltpu.SemaphoreType.DMA((turns, n_parts, hops))
    flat = pltpu.SemaphoreType.DMA((groups - 1,))
    return pl.pallas_call(
        functools.partial(scan_kernel, dims, local * groups),
        out_shape=(
            jax.ShapeDtypeStruct((turns, own, width), F32),
            jax.ShapeDtypeStruct((turns, own, LANES), F32),
            jax.ShapeDtypeStruct((rows, LANES), F32),
        ),
        in_specs=[vmem] * 6,
        out_specs=(vmem, vmem, vmem),
        scratch_shapes=[
            pltpu.VMEM((n_traits, local), BF16),
            pltpu.VMEM((local, width), BF16),
            pltpu.VMEM((local, width), BF16),
            pltpu.VMEM((turns, n_parts) + dims + (share, width), F32),
            pltpu.VMEM((groups, rows, LANES), F32),
            flat,
            flat,
            sems,
            sems,
            *bufs,
        ],
        compiler_params=pltpu.CompilerParams(
            collective_id=1, has_side_effects=True, vmem_limit_bytes=60 * 1024 * 1024
        ),
        name="scan",
    )(design, traits, genotypes, coef_t, coef_g, orders)


def cholesky_solve(factor, rhs):
    first = lax.linalg.triangular_solve(factor, rhs, left_side=True, lower=True)
    return lax.linalg.triangular_solve(factor, first, left_side=True, lower=True, transpose_a=True)


def shards(traits, covariates, genotypes, shuffles):
    groups = lax.axis_size("samp")
    me = lax.axis_index("samp")
    local, n_traits = traits.shape
    width = genotypes.shape[1]
    samples = local * groups
    used = covariates.shape[1] + 1
    rows = -(-used // 16) * 16
    wide = -(-used // LANES) * LANES
    ones = jnp.ones((local, 1), BF16)
    design = jnp.concatenate([ones, covariates, jnp.zeros((local, wide - used), BF16)], axis=1)
    design_t = design[:, :rows].T
    sums = cross_products(design_t, design, traits, genotypes, groups)
    gram = sums[:used, n_traits + width : n_traits + width + used]
    coef = cholesky_solve(jnp.linalg.cholesky(gram), sums[:used, : n_traits + width]).astype(BF16)
    coef = jnp.pad(coef, ((0, wide - used), (0, 0)))
    own_order = shuffles - me * local
    orders = jnp.concatenate([jnp.arange(local, dtype=jnp.int32)[None], own_order], axis=0)
    scores, peaks, squares = scan(
        design, traits, genotypes, coef[:, :n_traits], coef[:, n_traits:], orders, groups
    )
    own = n_traits // groups
    mine = lax.dynamic_slice_in_dim(squares.reshape(-1), me * own, own, 0)
    gain = lax.rsqrt(mine / samples + epsilon) * (math.sqrt(samples - used - 1) / samples)
    observed = scores[0] * gain[:, None]
    perm_max = lax.pmax(peaks[1:, :, 0] * gain[None, :], "tile")
    return (observed, perm_max)


def solution(mesh):
    placed = (P("samp", None), P("samp", None), P("samp", "tile"), P(None, "samp"))
    return jax.shard_map(
        shards,
        mesh=mesh,
        in_specs=placed,
        out_specs=(P("samp", "tile"), P(None, "samp")),
        check_vma=False,
    )
```

time: 422 us -> 131 us (0.31)
  waiting for transfers between devices: 216 us -> 0 us
  blocking collectives: 125 us -> 3.06 us
  Pallas kernels: 0 us -> 109 us
  local copies, waits for them, and re-layouts: 33 us -> 5.12 us
  matrix products: 23.5 us -> 1.63 us
  between operations: 14.3 us -> 0.74 us
    psum x2 -> x0, waiting for transfers between devices: 216 us -> none  [the longest x1 190 us: owned_scores(): summed = lax.psum(cross_local(trait_rows, rg_rows), 'samp')]
    psum x2 -> x0, blocking collectives: 123 us -> none  [the longest x1 78.7 us: shards(): gram, xty, xtg = lax.psum((gram, xty, xtg), 'samp')]
    pallas_call x0 -> x2, Pallas kernels: none -> 109 us  [the longest x1 83.2 us: scan(): pl.pallas_call(functools.partial(scan_kernel, dims, local * groups), out_...]
    gather x6 -> x0, local copies, waits for them, and re-layouts: 32.2 us -> none  [shards(): shuffled = jnp.take(rt_rows, local_order, axis=0)]
    dot_general x12 -> x0, matrix products: 21.5 us -> none  [the longest x10 18.7 us: cross_local(): lax.dot_general(left, right, (((0,), (0,)), ((), ())), preferred_element_...]
  transfers between devices with their start and end apart: 2 -> 0, of which waited for: 2 -> 0; matrix products, arithmetic and copies ran while one was open for 2% -> 0% of each run, Pallas kernels for 0% -> 0%
where the time goes in v1:
time: 131 us
  Pallas kernels  109 us (83%)
  other arithmetic  11.4 us (9%)
  local copies, waits for them, and re-layouts  5.12 us (4%)
  blocking collectives  3.06 us (2%)
  matrix products  1.63 us (1%)
    pallas_call x1, Pallas kernels, scan(): pl.pallas_call(functools.partial(scan_kernel, dims, local * groups), out_...  83.2 us
    pallas_call x1, Pallas kernels, cross_products(): pl.pallas_call(functools.partial(gram_kernel, groups), out_shape=jax.Shap...  25.4 us
    another operation x3, other arithmetic, shards(): jnp.linalg.cholesky(gram)  3.68 us
    another operation x2, other arithmetic, cholesky_solve(): lax.linalg.triangular_solve(factor, first, left_side=True, lower=True, tr...  3.18 us
    pmax x1, blocking collectives, shards(): perm_max = lax.pmax(peaks[1:, :, 0] * gain[None, :], 'tile')  3.06 us

profile of v1, /device:TPU:0, one launch (start us, length us, event | category | flops | bytes accessed | tf_op | source)
XLA Modules:
  0.0 130.5 jit_solution(5059321059576989652)
XLA Ops:
  0.7 0.1 pad.9.clone
  0.7 0.8 broadcast_subtract_fusion
  1.5 0.6 pad_add_fusion.order_ref
  2.1 1.0 copy.10
  3.1 0.1 maximum_maximum_fusion.d_ref
  3.3 0.0 copy-start
  3.3 0.8 copy.11.dt_ref
  4.1 0.0 copy-done
  4.1 25.4 %gram.1 = f32[48,1408]{1,0:T(8,128)} custom-call(bf16[48,1024]{1,0:T(8,128)(2,1)} %copy.11.dt_ref, bf16[1024,128]{1,0:T(8,128)(2,1)} %copy-done, bf16[1024,1024]{1,0:T(8,128)(2,1)} %t_ref.3, s32[1024,256]{1,0:T(8,128)} %g_ref.3), custom_call_target="tpu_custom_call" | custom-call | tf_op jit(solution)/shard_map/gram/pallas_call | solution.py:105
  29.5 0.7 slice.35
  30.2 0.1 copy.14
  30.3 0.7 fusion.5
  31.1 3.0 %cholesky.16 = f32[33,33]{1,0:T(8,128)S(1)} custom-call(f32[33,33]{1,0:T(8,128)S(1)} %fusion.5), custom_call_target="Cholesky" | custom-call | tf_op jit(solution)/shard_map/jit(cholesky)/cholesky | solution.py:356
  34.1 0.6 compare_reduce_fusion
  34.7 0.7 fusion.2
  35.4 2.5 %custom-call.8 = f32[1,33,33]{1,2,0:T(8,128)S(1)} custom-call(f32[1,33,33]{2,1,0:T(8,128)S(1)} %fusion.2), custom_call_target="InvertDiagBlocksLowerTriangular" | custom-call | tf_op jit(solution)/shard_map/triangular_solve | solution.py:339
  37.9 1.3 %fusion = f32[33,1280]{1,0:T(8,128)S(1)} fusion(f32[48,1408]{1,0:T(8,128)} %gram.1, f32[1,33,33]{1,2,0:T(8,128)S(1)} %custom-call.8), kind=kOutput, calls=%fused_computation.5 | convolution fusion | flops 16727040 | bytes 378116 | tf_op jit(solution)/shard_map/triangular_solve | solution.py:338
  39.3 0.3 convolution_convert_fusion
  39.6 0.6 pad_slice_fusion.cg_ref
  40.2 0.7 pad_slice_fusion.1.ct_ref
  40.9 83.2 %scan.1 = (f32[7,64,256]{2,1,0:T(8,128)}, f32[7,64,128]{2,1,0:T(8,128)}, f32[16,128]{1,0:T(8,128)}) custom-call(bf16[1024,128]{1,0:T(8,128)(2,1)} %copy-done, bf16[1024,1024]{1,0:T(8,128)(2,1)} %t_ref.3, s32[1024,256]{1,0:T(8,128)} %g_ref.3, bf16[128,1024]{1,0:T(8,128)(2,1)} %pad_slice_fusion.1.ct_ref, bf16[128,256]{1,0:T(8,128)(2,1)} %pad_slice_fusion.cg_ref, ...), custom_call_target="tpu_custom_call" | custom-call | tf_op jit(solution)/shard_map/scan/pallas_call | solution.py:309
  124.1 0.8 rsqrt_multiply_fusion
  124.9 1.5 %bitcast_multiply_fusion = f32[64,256]{1,0:T(8,128)} fusion(f32[7,64,256]{2,1,0:T(8,128)} %get-tuple-element.5, f32[64]{0:T(128)S(1)} %rsqrt_multiply_fusion), kind=kLoop, calls=%fused_computation.8 | loop fusion | flops 16384 | bytes 131328 | tf_op jit(solution)/shard_map/mul | solution.py:366
  126.4 1.0 slice_reduce_fusion
  127.5 3.1 %pmax.7 = f32[6,64]{1,0:T(8,128)} all-reduce(f32[6,64]{1,0:T(8,128)S(1)} %broadcast_multiply_fusion), channel_id=1, replica_groups=mesh['samp'=16,'tile'=2] {'tile'}, use_global_device_ids=true, to_apply=%region_2.3 | all-reduce | flops 384 | bytes 3072 | tf_op jit(solution)/shard_map/pmax | solution.py:367
  (6 shorter events, 0.1 us)
Async XLA Ops:
  3.3 0.8 copy-start

commit v2 on v1

v2 whole, which is shorter than its diff:
```python
import functools
import math

import jax
import jax.numpy as jnp
from jax import lax
from jax.experimental import pallas as pl
from jax.experimental.pallas import tpu as pltpu
from jax.sharding import PartitionSpec as P

MESH = pl.DeviceIdType.MESH
LANES = 128
F32, BF16 = jnp.float32, jnp.bfloat16
epsilon = 1e-05

ORDERS = ((2, 1, 0), (1, 2, 0))


def grid_of(groups):
    x = 4 if groups % 32 == 0 else 2
    y = 2
    return (groups // (x * y), y, x)


def start_all(copies):
    for copy in copies:
        copy.start()
    return copies


def scan_kernel(
    dims, tiles, samples, used, t_ref, c_ref, g_ref, order_ref, score_ref, peak_ref,
    design, parts, landed, mine, full, rhs, coef, rt, rg, moved, prod, found, squares, column,
    peaks, sum_sems, sq_send, sq_recv, tile_send, tile_recv, send, recv, *bufs
):
    groups = dims[0] * dims[1] * dims[2]
    me = lax.axis_index("samp")
    my_tile = lax.axis_index("tile")
    here = (me // (dims[1] * dims[2]), lax.rem(me // dims[2], dims[1]), lax.rem(me, dims[2]))
    turns, n_parts = prod.shape[0], prod.shape[1]
    share, width = prod.shape[5], prod.shape[6]
    local, traits = t_ref.shape
    own = traits // groups
    rows = coef.shape[0]
    quota = parts.shape[0] // groups
    strips = -(-used // 8)

    barrier = pltpu.get_barrier_semaphore()
    for d in range(1, groups):
        pl.semaphore_signal(
            barrier, inc=1, device_id={"samp": lax.rem(me + d, groups)}, device_id_type=MESH
        )
    for d in range(1, tiles):
        pl.semaphore_signal(
            barrier, inc=1, device_id={"tile": lax.rem(my_tile + d, tiles)}, device_id_type=MESH
        )

    lane = lax.broadcasted_iota(jnp.int32, design.shape, 1)
    design[...] = jnp.where(lane == used - 1, 1.0, 0.0).astype(BF16)
    design[:, : used - 1] = c_ref[...]
    design_t = design[...].T
    slot = 0
    for block_ref in (t_ref, g_ref, design):
        block = block_ref[...]
        if block.dtype != BF16:
            block = block.astype(F32).astype(BF16)
        block = jnp.dot(design_t, block, preferred_element_type=F32)
        for c in range(block.shape[1] // LANES):
            for r in range(strips):
                parts[slot] = block[8 * r : 8 * r + 8, LANES * c : LANES * c + LANES]
                slot += 1
    for i in range(slot, parts.shape[0]):
        parts[i] = jnp.zeros((8, LANES), F32)
    pl.semaphore_wait(barrier, groups + tiles - 2)

    def sum_copy(d, source, target, stage):
        return pltpu.make_async_remote_copy(
            src_ref=source,
            dst_ref=target,
            send_sem=sum_sems.at[2 * stage, d - 1],
            recv_sem=sum_sems.at[2 * stage + 1, d - 1],
            device_id={"samp": lax.rem(me + d, groups)},
            device_id_type=MESH,
        )

    scattered = start_all(
        [
            sum_copy(
                d, parts.at[pl.ds(lax.rem(me + d, groups) * quota, quota)], landed.at[d - 1], 0
            )
            for d in range(1, groups)
        ]
    )
    total = parts[pl.ds(me * quota, quota)]
    for d in range(1, groups):
        scattered[d - 1].wait_recv()
        total = total + landed[d - 1]
    mine[...] = total
    full[pl.ds(me * quota, quota)] = total
    gathered = start_all(
        [sum_copy(d, mine, full.at[pl.ds(me * quota, quota)], 1) for d in range(1, groups)]
    )
    rhs[...] = jnp.zeros(rhs.shape, F32)
    for copy in gathered:
        copy.wait_recv()

    n_t, n_g = traits // LANES, width // LANES
    half = rows // 2
    for c in range(n_t + n_g):
        for r in range(strips):
            rhs[half + 8 * r : half + 8 * r + 8, LANES * c : LANES * c + LANES] = full[
                c * strips + r
            ]
    gram = jnp.concatenate([full[(n_t + n_g) * strips + r] for r in range(strips)], axis=0)
    sub = lax.broadcasted_iota(jnp.int32, gram.shape, 0)
    lane = lax.broadcasted_iota(jnp.int32, gram.shape, 1)
    gram = jnp.where(lane == sub + half, 1.0, gram)
    for j in range(used):
        row = gram[j : j + 1, :] * (1.0 / gram[j : j + 1, j : j + 1])
        gram = jnp.where(sub == j, row, gram - gram[:, j : j + 1] * row)
    inverse = jnp.where(lane >= half, gram, 0.0)
    coef[...] = jnp.zeros(coef.shape, BF16)
    coef[: 8 * strips, :] = jnp.dot(
        inverse, rhs[...], precision=lax.Precision.HIGHEST, preferred_element_type=F32
    ).astype(BF16)

    step = min(256, local)
    sq_t = jnp.zeros((1, traits), F32)
    sq_g = jnp.zeros((1, width), F32)
    for i in range(local // step):
        at = slice(i * step, (i + 1) * step)
        d = design[at, :]
        resid = t_ref[at, :].astype(F32) - jnp.dot(
            d, coef[:, :traits], preferred_element_type=F32
        )
        sq_t = sq_t + jnp.sum(resid * resid, axis=0, keepdims=True)
        rt[:, at] = resid.astype(BF16).T
        dose = g_ref[at, :].astype(F32)
        resid = dose - jnp.dot(d, coef[:, traits:], preferred_element_type=F32)
        sq_g = sq_g + jnp.sum(resid * resid, axis=0, keepdims=True)
        rg[at, :] = resid.astype(BF16)
    squares[0] = jnp.zeros(squares.shape[1:], F32)
    for c in range(n_t):
        squares[0, c : c + 1, :] = sq_t[:, c * LANES : (c + 1) * LANES]
    for c in range(n_g):
        squares[0, n_t + c : n_t + c + 1, :] = sq_g[:, c * LANES : (c + 1) * LANES]

    def square_copy(d):
        return pltpu.make_async_remote_copy(
            src_ref=squares.at[0],
            dst_ref=squares.at[d],
            send_sem=sq_send.at[d - 1],
            recv_sem=sq_recv.at[d - 1],
            device_id={"samp": lax.rem(me + d, groups)},
            device_id_type=MESH,
        )

    def spot(axis, d):
        j = lax.rem(here[axis] + d, dims[axis])
        at = list(here)
        at[axis] = j
        return j, (at[0] * dims[1] + at[1]) * dims[2] + at[2]

    def pick(axis, order, stage, j):
        left = [a for a in (0, 1, 2) if a not in order[:stage]]
        return tuple(j if a == axis else slice(None) for a in left)

    def source(k, p, stage):
        if stage == 0:
            return prod.at[k, p]
        return bufs[5 * p + 2 * stage - 1].at[k]

    def copies(k, p, stage):
        order = ORDERS[p]
        axis = order[stage]
        first = sum(dims[a] - 1 for a in order[:stage])
        out = []
        for d in range(1, dims[axis]):
            j, peer = spot(axis, d)
            out.append(
                pltpu.make_async_remote_copy(
                    src_ref=source(k, p, stage).at[pick(axis, order, stage, j)],
                    dst_ref=bufs[5 * p + 2 * stage].at[k, d - 1],
                    send_sem=send.at[k, p, first + d - 1],
                    recv_sem=recv.at[k, p, first + d - 1],
                    device_id={"samp": peer},
                    device_id_type=MESH,
                )
            )
        return out

    def begin(k, stage):
        for p in range(n_parts):
            for copy in copies(k, p, stage):
                copy.start()

    def collect(k, stage):
        for p in range(n_parts):
            order = ORDERS[p]
            axis = order[stage]
            for copy in copies(k, p, stage):
                copy.wait_recv()
            total = source(k, p, stage)[pick(axis, order, stage, here[axis])]
            for d in range(1, dims[axis]):
                total = total + bufs[5 * p + 2 * stage][k, d - 1]
            if stage < 2:
                bufs[5 * p + 2 * stage + 1][k] = total
            else:
                found[k, p * share : (p + 1) * share, :] = total

    def multiply(k):
        @pl.when(k == 0)
        def _():
            moved[...] = rg[...]

        @pl.when(k > 0)
        def _():
            order = order_ref[pl.ds(k - 1, 1), :] - me * local
            for i in range(local // step):
                row = lax.broadcasted_iota(jnp.int32, (step, local), 0) + i * step
                hot = jnp.where(row == order, 1.0, 0.0).astype(BF16)
                moved[i * step : (i + 1) * step, :] = jnp.dot(
                    hot, rg[...], preferred_element_type=F32
                ).astype(BF16)

        depth = traits // dims[0]
        for z in range(dims[0]):
            block = jnp.dot(
                rt[z * depth : (z + 1) * depth, :], moved[...], preferred_element_type=F32
            ).reshape(dims[1], dims[2], n_parts, share, width)
            for p in range(n_parts):
                prod[k, p, z] = block[:, :, p]

    def turn(t, carry):
        @pl.when(t < turns)
        def _():
            multiply(t)
            begin(t, 0)

        @pl.when(t == 0)
        def _():
            for d in range(1, groups):
                square_copy(d).start()

        for stage in range(3):
            k = t - 1 - stage

            @pl.when(jnp.logical_and(k >= 0, k < turns))
            def _():
                collect(k, stage)
                if stage < 2:
                    begin(k, stage + 1)

        return carry

    lax.fori_loop(0, turns + 3, turn, 0)

    total = squares[0]
    for d in range(1, groups):
        square_copy(d).wait_recv()
        total = total + squares[d]
    gain = lax.rsqrt(total / samples + epsilon)
    factor = math.sqrt(samples - used - 1) / samples
    gain_g = jnp.concatenate([gain[n_t + c : n_t + c + 1, :] for c in range(n_g)], axis=1)
    turned = gain.T
    pos = lax.broadcasted_iota(jnp.int32, turned.shape, 1)
    chosen = jnp.sum(
        jnp.where(pos == me * own // LANES, turned, 0.0), axis=1, keepdims=True
    )
    column[...] = jnp.broadcast_to(chosen * factor, column.shape)
    gain_t = column[pl.ds(pl.multiple_of(lax.rem(me * own, LANES), 8), own), :]
    gain_t = gain_t[:, :1]
    score_ref[...] = found[0] * gain_g * gain_t
    top = jnp.zeros((own, LANES), F32)
    pos = lax.broadcasted_iota(jnp.int32, top.shape, 1)
    for k in range(1, turns):
        peak = jnp.max(jnp.abs(found[k] * gain_g), axis=1, keepdims=True) * gain_t
        top = jnp.where(pos == k - 1, peak, top)
    peaks[0] = top
    crossed = start_all(
        [
            pltpu.make_async_remote_copy(
                src_ref=peaks.at[0],
                dst_ref=peaks.at[d],
                send_sem=tile_send.at[d - 1],
                recv_sem=tile_recv.at[d - 1],
                device_id={"tile": lax.rem(my_tile + d, tiles)},
                device_id_type=MESH,
            )
            for d in range(1, tiles)
        ]
    )
    for copy in scattered + gathered:
        copy.wait_send()

    def finish(k, carry):
        for p in range(n_parts):
            for stage in range(3):
                for copy in copies(k, p, stage):
                    copy.wait_send()
        return carry

    lax.fori_loop(0, turns, finish, 0)
    for d in range(1, groups):
        square_copy(d).wait_send()
    for d in range(1, tiles):
        crossed[d - 1].wait()
        top = jnp.maximum(top, peaks[d])
    peak_ref[...] = top


def scan(traits, covariates, genotypes, shuffles):
    groups, tiles = lax.axis_size("samp"), lax.axis_size("tile")
    dims = grid_of(groups)
    turns = shuffles.shape[0] + 1
    local, n_traits = traits.shape
    width = genotypes.shape[1]
    used = covariates.shape[1] + 1
    own = n_traits // groups
    n_parts = len(ORDERS)
    share = own // n_parts
    bufs = []
    for order in ORDERS:
        left = [0, 1, 2]
        for stage, axis in enumerate(order):
            left.remove(axis)
            rest = tuple(dims[a] for a in left) + (share, width)
            bufs.append(pltpu.VMEM((turns, dims[axis] - 1) + rest, F32))
            if stage < 2:
                bufs.append(pltpu.VMEM((turns,) + rest, F32))
    hops = sum(n - 1 for n in dims)
    rows = -(-(n_traits + width) // (8 * LANES)) * 8
    strips = -(-used // 8)
    quota = -(-strips * ((n_traits + width) // LANES + 1) // groups)
    vmem = pl.BlockSpec(memory_space=pltpu.VMEM)
    sems = pltpu.SemaphoreType.DMA((turns, n_parts, hops))
    flat = pltpu.SemaphoreType.DMA((groups - 1,))
    pair = pltpu.SemaphoreType.DMA((max(tiles - 1, 1),))
    return pl.pallas_call(
        functools.partial(scan_kernel, dims, tiles, local * groups, used),
        out_shape=(
            jax.ShapeDtypeStruct((own, width), F32),
            jax.ShapeDtypeStruct((own, LANES), F32),
        ),
        in_specs=[vmem] * 4,
        out_specs=(vmem, vmem),
        scratch_shapes=[
            pltpu.VMEM((local, LANES), BF16),
            pltpu.VMEM((quota * groups, 8, LANES), F32),
            pltpu.VMEM((groups - 1, quota, 8, LANES), F32),
            pltpu.VMEM((quota, 8, LANES), F32),
            pltpu.VMEM((quota * groups, 8, LANES), F32),
            pltpu.VMEM((LANES, n_traits + width), F32),
            pltpu.VMEM((LANES, n_traits + width), BF16),
            pltpu.VMEM((n_traits, local), BF16),
            pltpu.VMEM((local, width), BF16),
            pltpu.VMEM((local, width), BF16),
            pltpu.VMEM((turns, n_parts) + dims + (share, width), F32),
            pltpu.VMEM((turns, own, width), F32),
            pltpu.VMEM((groups, rows, LANES), F32),
            pltpu.VMEM((LANES, LANES), F32),
            pltpu.VMEM((tiles, own, LANES), F32),
            pltpu.SemaphoreType.DMA((4, groups - 1)),
            flat,
            flat,
            pair,
            pair,
            sems,
            sems,
            *bufs,
        ],
        compiler_params=pltpu.CompilerParams(
            collective_id=0, has_side_effects=True, vmem_limit_bytes=60 * 1024 * 1024
        ),
        name="scan",
    )(traits, covariates, genotypes, shuffles)


def shards(traits, covariates, genotypes, shuffles):
    observed, peaks = scan(traits, covariates, genotypes, shuffles)
    return (observed, peaks[:, : shuffles.shape[0]].T)


def solution(mesh):
    placed = (P("samp", None), P("samp", None), P("samp", "tile"), P(None, "samp"))
    return jax.shard_map(
        shards,
        mesh=mesh,
        in_specs=placed,
        out_specs=(P("samp", "tile"), P(None, "samp")),
        check_vma=False,
    )
```

time: 131 us -> 108 us (0.82)
  other arithmetic: 11.4 us -> 0 us
  Pallas kernels: 109 us -> 102 us
  blocking collectives: 3.06 us -> 0 us
  matrix products: 1.63 us -> 0 us
    another operation x5 -> x0, other arithmetic: 6.86 us -> none  [the longest x3 3.68 us: shards(): jnp.linalg.cholesky(gram)]
    pallas_call x2 -> x1, Pallas kernels: 109 us -> 102 us  [scan(): pl.pallas_call(functools.partial(scan_kernel, dims, tiles, local * groups...]
    slice x4 -> x0, local copies, waits for them, and re-layouts: 3.14 us -> none  [the longest x1 1.05 us: shards(): perm_max = lax.pmax(peaks[1:, :, 0] * gain[None, :], 'tile')]
    pmax x1 -> x0, blocking collectives: 3.06 us -> none  [shards(): perm_max = lax.pmax(peaks[1:, :, 0] * gain[None, :], 'tile')]
    unnamed x4 -> x3, local copies, waits for them, and re-layouts: 1.1 us -> 3.81 us
    mul x3 -> x0, other arithmetic: 2.32 us -> none  [the longest x1 1.55 us: shards(): observed = scores[0] * gain[:, None]]
    another operation x2 -> x0, matrix products: 1.63 us -> none  [the longest x1 1.32 us: cholesky_solve(): first = lax.linalg.triangular_solve(factor, rhs, left_side=True, lower=True)]
where the time goes in v2:
time: 108 us
  Pallas kernels  102 us (94%)
  local copies, waits for them, and re-layouts  4.57 us (4%)
    pallas_call x1, Pallas kernels, scan(): pl.pallas_call(functools.partial(scan_kernel, dims, tiles, local * groups...  102 us
    unnamed x3, local copies, waits for them, and re-layouts  3.81 us

profile of v2, /device:TPU:0, one launch (start us, length us, event | category | flops | bytes accessed | tf_op | source)
XLA Modules:
  0.0 107.5 jit_solution(14534738371134096079)
XLA Ops:
  0.6 1.7 %copy.6.c_ref = bf16[1024,32]{1,0:T(8,128)(2,1)} copy(bf16[1024,32]{0,1:T(8,128)(2,1)} %param.5) | data formatting | bytes 131072 | tf_op args[1]
  2.3 102.3 %scan.1 = (f32[64,256]{1,0:T(8,128)}, f32[64,128]{1,0:T(8,128)}) custom-call(bf16[1024,1024]{1,0:T(8,128)(2,1)} %t_ref.1, bf16[1024,32]{1,0:T(8,128)(2,1)} %copy.6.c_ref, s32[1024,256]{1,0:T(8,128)} %g_ref.1, s32[6,1024]{1,0:T(8,128)} %order_ref.1), custom_call_target="tpu_custom_call" | custom-call | tf_op jit(solution)/shard_map/scan/pallas_call | solution.py:339
  104.6 0.8 slice_bitcast_fusion
  105.4 0.7 copy.7
  106.0 1.5 %copy.9 = f32[64,256]{1,0:T(8,128)} copy(f32[64,256]{1,0:T(8,128)} %get-tuple-element.10) | data formatting | bytes 131072

commit v3 on v2

--- a/solution.py
+++ b/solution.py
@@ -13,7 +13,13 @@
 F32, BF16 = jnp.float32, jnp.bfloat16
 epsilon = 1e-05
 
-ORDERS = ((2, 1, 0), (1, 2, 0))
+def parts_of(own, width):
+    cut, half = own - max(8, own // 64 * 8), width // 2
+    return (
+        ((2, 1, 0), slice(0, cut), slice(0, half)),
+        ((1, 2, 0), slice(0, cut), slice(half, width)),
+        ((0, 2, 1), slice(cut, own), slice(0, width)),
+    )
 
 
 def grid_of(groups):
@@ -29,21 +35,19 @@
 
 
 def scan_kernel(
-    dims, tiles, samples, used, t_ref, c_ref, g_ref, order_ref, score_ref, peak_ref,
-    design, parts, landed, mine, full, rhs, coef, rt, rg, moved, prod, found, squares, column,
+    dims, tiles, samples, used, areas, t_ref, c_ref, g_ref, order_ref, score_ref, peak_ref,
+    design, parts, landed, mine, full, rhs, coef, rt, rg, moved, found, squares, column,
     peaks, sum_sems, sq_send, sq_recv, tile_send, tile_recv, send, recv, *bufs
 ):
     groups = dims[0] * dims[1] * dims[2]
     me = lax.axis_index("samp")
     my_tile = lax.axis_index("tile")
     here = (me // (dims[1] * dims[2]), lax.rem(me // dims[2], dims[1]), lax.rem(me, dims[2]))
-    turns, n_parts = prod.shape[0], prod.shape[1]
-    share, width = prod.shape[5], prod.shape[6]
+    turns, width, n_parts = found.shape[0], found.shape[2], len(areas)
     local, traits = t_ref.shape
     own = traits // groups
     rows = coef.shape[0]
     quota = parts.shape[0] // groups
-    strips = -(-used // 8)
 
     barrier = pltpu.get_barrier_semaphore()
     for d in range(1, groups):
@@ -58,7 +62,8 @@
     lane = lax.broadcasted_iota(jnp.int32, design.shape, 1)
     design[...] = jnp.where(lane == used - 1, 1.0, 0.0).astype(BF16)
     design[:, : used - 1] = c_ref[...]
-    design_t = design[...].T
+    strips = -(-used // 8)
+    design_t = design[...].T[: -(-used // 16) * 16]
     slot = 0
     for block_ref in (t_ref, g_ref, design):
         block = block_ref[...]
@@ -166,12 +171,10 @@
         return tuple(j if a == axis else slice(None) for a in left)
 
     def source(k, p, stage):
-        if stage == 0:
-            return prod.at[k, p]
-        return bufs[5 * p + 2 * stage - 1].at[k]
+        return bufs[6 * p + 2 * stage].at[k]
 
     def copies(k, p, stage):
-        order = ORDERS[p]
+        order = areas[p][0]
         axis = order[stage]
         first = sum(dims[a] - 1 for a in order[:stage])
         out = []
@@ -180,7 +183,7 @@
             out.append(
                 pltpu.make_async_remote_copy(
                     src_ref=source(k, p, stage).at[pick(axis, order, stage, j)],
-                    dst_ref=bufs[5 * p + 2 * stage].at[k, d - 1],
+                    dst_ref=bufs[6 * p + 2 * stage + 1].at[k, d - 1],
                     send_sem=send.at[k, p, first + d - 1],
                     recv_sem=recv.at[k, p, first + d - 1],
                     device_id={"samp": peer},
@@ -196,17 +199,17 @@
 
     def collect(k, stage):
         for p in range(n_parts):
-            order = ORDERS[p]
+            order = areas[p][0]
             axis = order[stage]
             for copy in copies(k, p, stage):
                 copy.wait_recv()
             total = source(k, p, stage)[pick(axis, order, stage, here[axis])]
             for d in range(1, dims[axis]):
-                total = total + bufs[5 * p + 2 * stage][k, d - 1]
+                total = total + bufs[6 * p + 2 * stage + 1][k, d - 1]
             if stage < 2:
-                bufs[5 * p + 2 * stage + 1][k] = total
+                bufs[6 * p + 2 * stage + 2][k] = total
             else:
-                found[k, p * share : (p + 1) * share, :] = total
+                found[k, areas[p][1], areas[p][2]] = total
 
     def multiply(k):
         @pl.when(k == 0)
@@ -227,9 +230,9 @@
         for z in range(dims[0]):
             block = jnp.dot(
                 rt[z * depth : (z + 1) * depth, :], moved[...], preferred_element_type=F32
-            ).reshape(dims[1], dims[2], n_parts, share, width)
+            ).reshape(dims[1], dims[2], own, width)
             for p in range(n_parts):
-                prod[k, p, z] = block[:, :, p]
+                bufs[6 * p][k, z] = block[:, :, areas[p][1], areas[p][2]]
 
     def turn(t, carry):
         @pl.when(t < turns)
@@ -306,7 +309,7 @@
     for d in range(1, tiles):
         crossed[d - 1].wait()
         top = jnp.maximum(top, peaks[d])
-    peak_ref[...] = top
+    peak_ref[...] = top.T[: turns - 1]
 
 
 def scan(traits, covariates, genotypes, shuffles):
@@ -317,14 +320,16 @@
     width = genotypes.shape[1]
     used = covariates.shape[1] + 1
     own = n_traits // groups
-    n_parts = len(ORDERS)
-    share = own // n_parts
+    areas = parts_of(own, width)
+    n_parts = len(areas)
     bufs = []
-    for order in ORDERS:
+    for order, part_rows, part_lanes in areas:
+        size = (part_rows.stop - part_rows.start, part_lanes.stop - part_lanes.start)
         left = [0, 1, 2]
+        bufs.append(pltpu.VMEM((turns,) + dims + size, F32))
         for stage, axis in enumerate(order):
             left.remove(axis)
-            rest = tuple(dims[a] for a in left) + (share, width)
+            rest = tuple(dims[a] for a in left) + size
             bufs.append(pltpu.VMEM((turns, dims[axis] - 1) + rest, F32))
             if stage < 2:
                 bufs.append(pltpu.VMEM((turns,) + rest, F32))
@@ -337,10 +342,10 @@
     flat = pltpu.SemaphoreType.DMA((groups - 1,))
     pair = pltpu.SemaphoreType.DMA((max(tiles - 1, 1),))
     return pl.pallas_call(
-        functools.partial(scan_kernel, dims, tiles, local * groups, used),
+        functools.partial(scan_kernel, dims, tiles, local * groups, used, areas),
         out_shape=(
             jax.ShapeDtypeStruct((own, width), F32),
-            jax.ShapeDtypeStruct((own, LANES), F32),
+            jax.ShapeDtypeStruct((turns - 1, own), F32),
         ),
         in_specs=[vmem] * 4,
         out_specs=(vmem, vmem),
@@ -355,7 +360,6 @@
             pltpu.VMEM((n_traits, local), BF16),
             pltpu.VMEM((local, width), BF16),
             pltpu.VMEM((local, width), BF16),
-            pltpu.VMEM((turns, n_parts) + dims + (share, width), F32),
             pltpu.VMEM((turns, own, width), F32),
             pltpu.VMEM((groups, rows, LANES), F32),
             pltpu.VMEM((LANES, LANES), F32),
@@ -377,8 +381,7 @@
 
 
 def shards(traits, covariates, genotypes, shuffles):
-    observed, peaks = scan(traits, covariates, genotypes, shuffles)
-    return (observed, peaks[:, : shuffles.shape[0]].T)
+    return scan(traits, covariates, genotypes, shuffles)
 
 
 def solution(mesh):

time: 108 us -> 101 us (0.935)
  Pallas kernels: 102 us -> 95.6 us
    pallas_call x1, Pallas kernels: 102 us -> 95.6 us  [scan(): pl.pallas_call(functools.partial(scan_kernel, dims, tiles, local * groups...]
where the time goes in v3:
time: 101 us
  Pallas kernels  95.6 us (95%)
  local copies, waits for them, and re-layouts  4.42 us (4%)
    pallas_call x1, Pallas kernels, scan(): pl.pallas_call(functools.partial(scan_kernel, dims, tiles, local * groups...  95.6 us
    unnamed x3, local copies, waits for them, and re-layouts  4.42 us

profile of v3, /device:TPU:0, one launch (start us, length us, event | category | flops | bytes accessed | tf_op | source)
XLA Modules:
  0.0 100.7 jit_solution(13379347590834996139)
XLA Ops:
  0.6 1.7 %copy.6.c_ref = bf16[1024,32]{1,0:T(8,128)(2,1)} copy(bf16[1024,32]{0,1:T(8,128)(2,1)} %param.5) | data formatting | bytes 131072 | tf_op args[1]
  2.3 95.6 %scan.1 = (f32[64,256]{1,0:T(8,128)}, f32[6,64]{1,0:T(8,128)}) custom-call(bf16[1024,1024]{1,0:T(8,128)(2,1)} %t_ref.1, bf16[1024,32]{1,0:T(8,128)(2,1)} %copy.6.c_ref, s32[1024,256]{1,0:T(8,128)} %g_ref.1, s32[6,1024]{1,0:T(8,128)} %order_ref.1), custom_call_target="tpu_custom_call" | custom-call | tf_op jit(solution)/shard_map/scan/pallas_call | solution.py:344
  98.0 1.5 %copy.9 = f32[64,256]{1,0:T(8,128)} copy(f32[64,256]{1,0:T(8,128)} %get-tuple-element.4) | data formatting | bytes 131072
  99.4 1.3 %copy.10 = f32[6,64]{1,0:T(8,128)} copy(f32[6,64]{1,0:T(8,128)} %get-tuple-element.5) | data formatting | bytes 3072
